TPU v7x, 32 devices: a whole 2x2x4 slice. The times are simulated.
32 devices in a mesh: groups: 2 (over y), seq: 16 (over z, x, core).
Axes of the slice: x: 2, y: 2, z: 4, core: 2. Of those that a mesh axis runs over, the one named last changes fastest.
Arguments:
- queries: bfloat16 [8192, 2048], P(('groups', 'seq')), parts along dimension 0, may hold values from -20 to 20
- keys: bfloat16 [8192, 2048], P(('groups', 'seq')), parts along dimension 0, may hold values from -20 to 20
- values: bfloat16 [8192, 2048], P(('groups', 'seq')), parts along dimension 0, may hold values from -6 to 6
- block_counts: int32 [16], P('groups'), parts along dimension 0, may hold values from 2 to 6, as said below
- last_tokens: int32 [32], P('groups'), parts along dimension 0, may hold values from 64 to 128
- pack_order: int32 [32], P('groups'), parts along dimension 0, may hold values from 0 to 15, as said below
- decode_slot: int32 [16], P('groups'), parts along dimension 0, may hold values from 0 to 7, each once
Outputs:
- attended: bfloat16 [8192, 2048], P(('groups', 'seq')), parts along dimension 0
- cache_keys: bfloat16 [32, 32, 128, 128], P(('groups', 'seq')), parts along dimension 0
- cache_values: bfloat16 [32, 32, 128, 128], P(('groups', 'seq')), parts along dimension 0
There are 2 independent parts, one for each index of `groups`. A program takes and returns all parts, laid end to end along the dimension named above; each array names one. Nothing has to cross between parts.
Inputs may be any that keep to these rules, and one draw needn't show every extreme that they name: `block_counts`: they sum to 24; the largest equals 6. `pack_order`: each prompt number appears once. The last 1 positions hold null prompts, and the position before them a conditional prompt of 6 blocks. `decode_slot`: each slot appears once.
All inputs are finite; a program needn't handle non-finite values.
Results may differ from a plain program's by a relative error of at most 0.0034.
Values may be sent and summed in bfloat16 or wider, within the bound.
A program may use at most 64 MiB of HBM per device.

v0:
```python
import jax
import jax.numpy as jnp
from jax import lax
from jax.sharding import PartitionSpec as P

HEADS = 16
HEAD_DIM = 128
BLOCK = 128
MAXB = 6
MASKED_SCORE = -1e30


def shifted(block, axis, distance):
    devices = range(lax.axis_size(axis))
    route = [(i - distance, i) for i in devices if i - distance in devices]
    return lax.ppermute(block, axis, route)


def block_tables(block_counts, last_tokens, pack_order, decode_slot, total_blocks, block):
    pair_count = block_counts.shape[0]
    prompts = 2 * pair_count
    prompt_ids = jnp.arange(prompts, dtype=jnp.int32)
    prompt_sizes = jnp.concatenate([block_counts, jnp.ones((pair_count,), jnp.int32)])
    picked = (pack_order[:, None] == prompt_ids[None, :]).astype(jnp.int32)
    packed_sizes = jnp.sum(picked * prompt_sizes[None, :], axis=1)
    packed_tails = jnp.sum(picked * last_tokens[None, :], axis=1)
    block_ends = jnp.cumsum(packed_sizes)
    starts = block_ends - packed_sizes
    blocks = jnp.arange(total_blocks, dtype=jnp.int32)
    member = (
        (starts[None, :] <= blocks[:, None]) & (blocks[:, None] < block_ends[None, :])
    ).astype(jnp.int32)
    position = jnp.sum(member * prompt_ids[None, :], axis=1)
    prompt = jnp.sum(member * pack_order[None, :], axis=1)
    within = blocks - jnp.sum(member * starts[None, :], axis=1)
    is_last = blocks + 1 == jnp.sum(member * block_ends[None, :], axis=1)
    valid_tokens = jnp.where(is_last, jnp.sum(member * packed_tails[None, :], axis=1), block)
    pair_ids = jnp.arange(pair_count, dtype=jnp.int32)
    earlier = (decode_slot[None, :] < decode_slot[:, None]).astype(jnp.int32)
    slot_start = jnp.sum(earlier * (block_counts + 1)[None, :], axis=1)
    pair_of = prompt % pair_count
    owner = (pair_of[:, None] == pair_ids[None, :]).astype(jnp.int32)
    base_slot = jnp.sum(owner * slot_start[None, :], axis=1)
    own_count = jnp.sum(owner * block_counts[None, :], axis=1)
    destination = base_slot + jnp.where(prompt >= pair_count, own_count, within)
    hits = (destination[None, :] == blocks[:, None]).astype(jnp.int32)
    source = jnp.sum(hits * blocks[None, :], axis=1)
    return (position, valid_tokens, source)


def hand_off(paired, source, devices):
    tokens_here = paired.shape[1]
    blocks_here = tokens_here // BLOCK
    splits = devices // HEADS
    slice_len = BLOCK // splits
    outgoing = paired.reshape(2, blocks_here, splits, slice_len, HEADS, HEAD_DIM)
    outgoing = jnp.transpose(outgoing, (4, 2, 0, 1, 3, 5)).reshape(
        devices, 2, blocks_here, slice_len, HEAD_DIM
    )
    arrived = lax.all_to_all(outgoing, "seq", split_axis=0, concat_axis=2, tiled=True)
    ordered = jnp.take(arrived[0], source, axis=1)
    return (ordered[0][None], ordered[1][None])


def attend(queries, paired, position, valid_tokens, own_index, reach):
    tokens_here, features = queries.shape
    blocks_here = tokens_here // BLOCK
    pieces = [paired]
    current = paired
    for distance in range(reach):
        current = shifted(current, "seq", 1)
        pieces.insert(0, current)
    prior_count = reach * blocks_here
    window = jnp.concatenate(pieces, axis=1)
    window_blocks = prior_count + blocks_here
    lead_blocks = reach * blocks_here
    padded_docs = jnp.concatenate([jnp.full((lead_blocks,), -1, jnp.int32), position])
    padded_valid = jnp.concatenate([jnp.zeros((lead_blocks,), jnp.int32), valid_tokens])
    first_block = own_index * blocks_here + lead_blocks - prior_count
    window_docs = lax.dynamic_slice_in_dim(padded_docs, first_block, window_blocks)
    window_valid = lax.dynamic_slice_in_dim(padded_valid, first_block, window_blocks)
    own_first = own_index * blocks_here
    query_docs = lax.dynamic_slice_in_dim(position, own_first, blocks_here)
    query_valid = lax.dynamic_slice_in_dim(valid_tokens, own_first, blocks_here)
    token_ids = jnp.arange(BLOCK, dtype=jnp.int32)
    key_docs = jnp.repeat(window_docs, BLOCK)
    key_limit = jnp.repeat(window_valid, BLOCK)
    key_tokens = jnp.tile(token_ids, window_blocks)
    key_order = jnp.arange(window_blocks * BLOCK, dtype=jnp.int32) - prior_count * BLOCK
    query_order = jnp.arange(tokens_here, dtype=jnp.int32)
    allowed = key_docs[None, :] == jnp.repeat(query_docs, BLOCK)[:, None]
    allowed = (
        allowed & (key_order[None, :] <= query_order[:, None]) & (key_tokens < key_limit)[None, :]
    )
    query_ok = jnp.tile(token_ids, blocks_here) < jnp.repeat(query_valid, BLOCK)
    score_scale = HEAD_DIM ** (-0.5)
    query_heads = jnp.moveaxis(queries.reshape(tokens_here, HEADS, HEAD_DIM), 1, 0)
    key_heads = jnp.moveaxis(window[0].reshape(-1, HEADS, HEAD_DIM), 1, 0)
    value_heads = jnp.moveaxis(window[1].reshape(-1, HEADS, HEAD_DIM), 1, 0)

    def one_head(operands):
        query_part, key_part, value_part = operands
        scores = (
            jnp.einsum("qd,kd->qk", query_part, key_part, preferred_element_type=jnp.float32)
            * score_scale
        )
        scores = jnp.where(allowed, scores, MASKED_SCORE)
        peak = jnp.max(scores, axis=1, keepdims=True)
        weights = jnp.exp(scores - peak)
        totals = jnp.sum(weights, axis=1, keepdims=True)
        mixed = jnp.dot(
            weights.astype(jnp.bfloat16), value_part, preferred_element_type=jnp.float32
        )
        return mixed / totals

    head_outputs = lax.map(one_head, (query_heads, key_heads, value_heads))
    merged = jnp.moveaxis(head_outputs, 0, 1).reshape(tokens_here, features)
    return jnp.where(query_ok[:, None], merged, 0.0).astype(jnp.bfloat16)


def local(queries, keys, values, block_counts, last_tokens, pack_order, decode_slot):
    devices = lax.axis_size("seq")
    own_index = lax.axis_index("seq")
    tokens_here = queries.shape[0]
    blocks_here = tokens_here // BLOCK
    reach = (MAXB + blocks_here - 2) // blocks_here
    position, valid_tokens, source = block_tables(
        block_counts, last_tokens, pack_order, decode_slot, blocks_here * devices, BLOCK
    )
    paired = jnp.stack([keys, values])
    attended = attend(queries, paired, position, valid_tokens, own_index, reach)
    cache_keys, cache_values = hand_off(paired, source, devices)
    return (attended, cache_keys, cache_values)


def solution(mesh):
    placed = (
        P(("groups", "seq"), None),
        P(("groups", "seq"), None),
        P(("groups", "seq"), None),
        P("groups"),
        P("groups"),
        P("groups"),
        P("groups"),
    )
    return jax.shard_map(
        local,
        mesh=mesh,
        in_specs=placed,
        out_specs=(
            P(("groups", "seq"), None),
            P(("groups", "seq"), None, None, None),
            P(("groups", "seq"), None, None, None),
        ),
        check_vma=False,
    )
```

profile of v0, /device:TPU:20, one launch (start us, length us, event | category | flops | bytes accessed | tf_op | source)
XLA Modules:
  0.0 189.0 jit_solution(15952049757768567406)
XLA Ops:
  0.6 1.6 copy.47
  2.8 1.5 pad_maximum_fusion
  4.2 1.9 %collective-permute-start = (bf16[2,256,2048]{1,2,0:T(8,128)(2,1)}, bf16[2,256,2048]{1,2,0:T(8,128)(2,1)}, u32[]{:S(2)}, u32[]{:S(2)}) collective-permute-start(bf16[2,256,2048]{1,2,0:T(8,128)(2,1)} %pad_maximum_fusion), channel_id=1, source_target_pairs={{0,1},{1,2},{2,3},{3,4},{4,5},{5,6},{6,7},{7,8},{8,9},{9,10},{10,1... | collective-permute-start | bytes 6291464 | tf_op jit(solution)/shard_map/ppermute | solution.py:16
  6.8 1.9 %copy.53 = bf16[16,2,2,128,128]{4,3,2,1,0:T(8,128)(2,1)} copy(bf16[16,2,2,128,128]{4,0,3,2,1:T(8,128)(2,1)S(1)} %maximum_bitcast_fusion) | data formatting | bytes 4194304 | tf_op jit(solution)/shard_map/reshape | solution.py:57
  8.8 6.6 %all-to-all-start = ((bf16[16,2,2,128,128]{4,3,2,1,0:T(8,128)(2,1)}), bf16[16,2,2,128,128]{4,3,2,1,0:T(8,128)(2,1)}, u32[]{:S(2)}, u32[]{:S(2)}) async-start(bf16[16,2,2,128,128]{4,3,2,1,0:T(8,128)(2,1)} %copy.53), calls=%async_computation | async-start | bytes 4194304 | tf_op jit(solution)/shard_map/all_to_all | solution.py:60
  15.4 51.1 %collective-permute-done = bf16[2,256,2048]{1,2,0:T(8,128)(2,1)} collective-permute-done((bf16[2,256,2048]{1,2,0:T(8,128)(2,1)}, bf16[2,256,2048]{1,2,0:T(8,128)(2,1)}, u32[]{:S(2)}, u32[]{:S(2)}) %collective-permute-start) | collective-permute-done | bytes 2097184 | tf_op jit(solution)/shard_map/ppermute | solution.py:16
  66.5 1.9 %collective-permute-start.1 = (bf16[2,256,2048]{1,2,0:T(8,128)(2,1)}, bf16[2,256,2048]{1,2,0:T(8,128)(2,1)}, u32[]{:S(2)}, u32[]{:S(2)}) collective-permute-start(bf16[2,256,2048]{1,2,0:T(8,128)(2,1)} %collective-permute-done), channel_id=1, source_target_pairs={{0,1},{1,2},{2,3},{3,4},{4,5},{5,6},{6,7},{7,8},{8,9},{9,10},{10,1... | collective-permute-start | bytes 6291464 | tf_op jit(solution)/shard_map/ppermute | solution.py:16
  69.5 30.8 %collective-permute-done.1 = bf16[2,256,2048]{1,2,0:T(8,128)(2,1)} collective-permute-done((bf16[2,256,2048]{1,2,0:T(8,128)(2,1)}, bf16[2,256,2048]{1,2,0:T(8,128)(2,1)}, u32[]{:S(2)}, u32[]{:S(2)}) %collective-permute-start.1) | collective-permute-done | bytes 2097184 | tf_op jit(solution)/shard_map/ppermute | solution.py:16
  100.3 1.9 %collective-permute-start.2 = (bf16[2,256,2048]{1,2,0:T(8,128)(2,1)}, bf16[2,256,2048]{1,2,0:T(8,128)(2,1)}, u32[]{:S(2)}, u32[]{:S(2)}) collective-permute-start(bf16[2,256,2048]{1,2,0:T(8,128)(2,1)} %collective-permute-done.1), channel_id=1, source_target_pairs={{0,1},{1,2},{2,3},{3,4},{4,5},{5,6},{6,7},{7,8},{8,9},{9,10},{10,1... | collective-permute-start | bytes 6291464 | tf_op jit(solution)/shard_map/ppermute | solution.py:16
  102.5 2.3 %copy.46 = bf16[256,2048]{0,1:T(8,128)(2,1)} copy(bf16[256,2048]{1,0:T(8,128)(2,1)} %param.9) | data formatting | bytes 2097152 | tf_op args[0]
  105.0 3.2 %copy.54 = bf16[16,2,2,128,128]{4,3,2,0,1:T(8,128)(2,1)} copy(bf16[16,2,2,128,128]{4,3,2,1,0:T(8,128)(2,1)} %all-to-all-done) | data formatting | bytes 4194304 | tf_op jit(solution)/shard_map/all_to_all | solution.py:60
  108.3 3.7 %gather_fusion = bf16[32,2,128,128]{3,2,1,0:T(8,128)(2,1)} fusion(bf16[2,32,128,128]{3,2,1,0:T(8,128)(2,1)} %bitcast.87, s32[1024]{0:T(1024)S(1)} %pad_clamp_fusion), kind=kCustom, calls=%fused_computation | custom fusion | bytes 4194432 | tf_op jit(solution)/shard_map/jit(_take)/gather | solution.py:61
  112.0 1.8 select_bitcast_fusion
  113.9 1.5 slice_bitcast_fusion
  115.3 13.6 %collective-permute-done.2 = bf16[2,256,2048]{1,2,0:T(8,128)(2,1)} collective-permute-done((bf16[2,256,2048]{1,2,0:T(8,128)(2,1)}, bf16[2,256,2048]{1,2,0:T(8,128)(2,1)}, u32[]{:S(2)}, u32[]{:S(2)}) %collective-permute-start.2) | collective-permute-done | bytes 2097184 | tf_op jit(solution)/shard_map/ppermute | solution.py:16
  128.9 3.9 %maximum_maximum_fusion = bf16[2,1024,2048]{1,2,0:T(8,128)(2,1)S(1)} fusion(bf16[1,256,2048]{1,2,0:T(8,128)(2,1)S(1)} %bitcast.86, bf16[1,256,2048]{1,2,0:T(8,128)(2,1)S(1)} %bitcast.84, bf16[2,256,2048]{1,2,0:T(8,128)(2,1)} %collective-permute-done, bf16[2,256,2048]{1,2,0:T(8,128)(2,1)} %collective-permute-done.1, ...), kind=kLoop, calls=%fused_computation.22 | loop fusion | flops 41943040 | bytes 16777216 | tf_op jit(solution)/shard_map/concatenate | solution.py:74
  132.8 3.7 %fusion.26 = (bf16[1,1024,2048]{1,2,0:T(8,128)(2,1)}, bf16[1,1024,2048]{1,2,0:T(8,128)(2,1)}) fusion(bf16[2,1024,2048]{1,2,0:T(8,128)(2,1)S(1)} %maximum_maximum_fusion), kind=kLoop, calls=%fused_computation.69 | loop fusion | bytes 16777216 | tf_op jit(solution)/shard_map/slice | solution.py:99
  136.4 51.3 %while.11 = (s32[]{:T(128)}, bf16[16,256,128]{2,1,0:T(8,128)(2,1)S(1)}, bf16[16,256,128]{1,2,0:T(8,128)(2,1)}, bf16[16,1024,128]{1,2,0:T(8,128)(2,1)}, bf16[16,1...) while((s32[]{:T(128)}, ...), condition=%wide.region_9.10_spmd.clone, body=%wide.region_6.0_spmd.clone.sunk | while | flops 137133568 | bytes 3884133 | solution.py:116
  136.4 1.5 fusion.35
  138.3 1.3 fusion.37
  139.6 1.5 fusion.35
  141.5 1.3 fusion.37
  142.9 1.5 fusion.35
  144.7 1.3 fusion.37
  146.1 1.5 fusion.35
  147.9 1.3 fusion.37
  149.3 1.5 fusion.35
  151.1 1.3 fusion.37
  152.5 1.5 fusion.35
  154.3 1.3 fusion.37
  155.7 1.5 fusion.35
  157.5 1.3 fusion.37
  158.9 1.5 fusion.35
  160.8 1.3 fusion.37
  162.1 1.5 fusion.35
  164.0 1.3 fusion.37
  165.3 1.5 fusion.35
  167.2 1.3 fusion.37
  168.5 1.5 fusion.35
  170.4 1.3 fusion.37
  171.7 1.5 fusion.35
  173.6 1.3 fusion.37
  174.9 1.5 fusion.35
  176.8 1.3 fusion.37
  178.1 1.5 fusion.35
  180.0 1.3 fusion.37
  181.4 1.5 fusion.35
  184.6 1.5 fusion.35
  (62 shorter events, 11.5 us)
Async XLA Ops:
  0.6 1.6 copy-start.1
  2.8 3.4 %copy-start = (bf16[256,2048]{1,0:T(8,128)(2,1)S(1)}, bf16[256,2048]{1,0:T(8,128)(2,1)}, u32[]{:S(2)}) copy-start(bf16[256,2048]{1,0:T(8,128)(2,1)} %param.10) | copy-start | bytes 3145732
  4.2 62.3 %collective-permute-start = (bf16[2,256,2048]{1,2,0:T(8,128)(2,1)}, bf16[2,256,2048]{1,2,0:T(8,128)(2,1)}, u32[]{:S(2)}, u32[]{:S(2)}) collective-permute-start(bf16[2,256,2048]{1,2,0:T(8,128)(2,1)} %pad_maximum_fusion), channel_id=1, source_target_pairs={{0,1},{1,2},{2,3},{3,4},{4,5},{5,6},{6,7},{7,8},{8,9},{9,10},{10,1... | collective-permute-start | bytes 6291464 | tf_op jit(solution)/shard_map/ppermute | solution.py:16
  8.8 59.6 %copy-start.5 = (s32[8]{0:T(128)S(1)}, s32[8]{0:T(128)}, u32[]{:S(2)}) copy-start(s32[8]{0:T(128)} %param.12) | copy-start | bytes 100
  8.8 59.7 %copy-start.2 = (s32[16]{0:T(128)S(1)}, s32[16]{0:T(128)}, u32[]{:S(2)}) copy-start(s32[16]{0:T(128)} %param.14) | copy-start | bytes 196
  8.8 59.7 %copy-start.4 = (s32[16]{0:T(128)S(1)}, s32[16]{0:T(128)}, u32[]{:S(2)}) copy-start(s32[16]{0:T(128)} %param.13) | copy-start | bytes 196
  8.8 60.3 %copy-start.3 = (s32[8]{0:T(128)S(1)}, s32[8]{0:T(128)}, u32[]{:S(2)}) copy-start(s32[8]{0:T(128)} %param.15) | copy-start | bytes 100
  8.8 96.2 %all-to-all-start = ((bf16[16,2,2,128,128]{4,3,2,1,0:T(8,128)(2,1)}), bf16[16,2,2,128,128]{4,3,2,1,0:T(8,128)(2,1)}, u32[]{:S(2)}, u32[]{:S(2)}) async-start(bf16[16,2,2,128,128]{4,3,2,1,0:T(8,128)(2,1)} %copy.53), calls=%async_computation | async-start | bytes 4194304 | tf_op jit(solution)/shard_map/all_to_all | solution.py:60
  66.5 33.8 %collective-permute-start.1 = (bf16[2,256,2048]{1,2,0:T(8,128)(2,1)}, bf16[2,256,2048]{1,2,0:T(8,128)(2,1)}, u32[]{:S(2)}, u32[]{:S(2)}) collective-permute-start(bf16[2,256,2048]{1,2,0:T(8,128)(2,1)} %collective-permute-done), channel_id=1, source_target_pairs={{0,1},{1,2},{2,3},{3,4},{4,5},{5,6},{6,7},{7,8},{8,9},{9,10},{10,1... | collective-permute-start | bytes 6291464 | tf_op jit(solution)/shard_map/ppermute | solution.py:16
  100.3 28.6 %collective-permute-start.2 = (bf16[2,256,2048]{1,2,0:T(8,128)(2,1)}, bf16[2,256,2048]{1,2,0:T(8,128)(2,1)}, u32[]{:S(2)}, u32[]{:S(2)}) collective-permute-start(bf16[2,256,2048]{1,2,0:T(8,128)(2,1)} %collective-permute-done.1), channel_id=1, source_target_pairs={{0,1},{1,2},{2,3},{3,4},{4,5},{5,6},{6,7},{7,8},{8,9},{9,10},{10,1... | collective-permute-start | bytes 6291464 | tf_op jit(solution)/shard_map/ppermute | solution.py:16
where the time goes:
time: 190 us; the launch traced here: 189 us
  waiting for transfers between devices  95.5 us (50%)
  matrix products  46.1 us (24%)
  local copies, waits for them, and re-layouts  19.4 us (10%)
  other arithmetic  14.5 us (8%)
  starting transfers between devices  12.3 us (6%)
    ppermute x3, waiting for transfers between devices, shifted(): return lax.ppermute(block, axis, route)  95.5 us
    dot_general x16, matrix products, one_head(): jnp.einsum('qd,kd->qk', query_part, key_part, preferred_element_type=jnp....  24.7 us
    dot_general x16, matrix products, one_head(): jnp.dot(weights.astype(jnp.bfloat16), value_part, preferred_element_type=...  21.4 us
    all_to_all x1, starting transfers between devices, hand_off(): lax.all_to_all(outgoing, 'seq', split_axis=0, concat_axis=2, tiled=True)  6.57 us
    unnamed x18, local copies, waits for them, and re-layouts  6.28 us
    ppermute x3, starting transfers between devices, shifted(): return lax.ppermute(block, axis, route)  5.73 us
    reduce_sum x16, other arithmetic, one_head(): totals = jnp.sum(weights, axis=1, keepdims=True)  4.88 us
    concatenate x1, other arithmetic, attend(): window = jnp.concatenate(pieces, axis=1)  3.88 us
  transfers between devices with their start and end apart: 4, of which 3 were waited for; matrix products, arithmetic and copies ran while one was open for 9% of the time, Pallas kernels for 0%

commit v1 on v0

--- a/solution.py
+++ b/solution.py
@@ -8,6 +8,28 @@
 BLOCK = 128
 MAXB = 6
 MASKED_SCORE = -1e30
+
+
+def _keep_up_series(content, join_dim, dim_k):
+    bus_axis = "seq"
+    upper, step_out = (lax.axis_size(bus_axis), lax.axis_index(bus_axis))
+    frame_out = content.shape[join_dim] // upper
+    heard = list(content.shape)
+    heard[join_dim] = frame_out
+    main = heard[dim_k]
+    heard[dim_k] = main * upper
+    v1 = jnp.zeros(heard, content.dtype)
+    for to_i in range(upper):
+        block_out = lax.dynamic_slice_in_dim(
+            content, (step_out ^ to_i) * frame_out, frame_out, axis=join_dim
+        )
+        if to_i:
+            items = []
+            for j0 in range(upper):
+                items.append((j0, j0 ^ to_i))
+            block_out = lax.ppermute(block_out, bus_axis, items)
+        v1 = lax.dynamic_update_slice_in_dim(v1, block_out, (step_out ^ to_i) * main, axis=dim_k)
+    return v1
 
 
 def shifted(block, axis, distance):
@@ -57,7 +79,7 @@
     outgoing = jnp.transpose(outgoing, (4, 2, 0, 1, 3, 5)).reshape(
         devices, 2, blocks_here, slice_len, HEAD_DIM
     )
-    arrived = lax.all_to_all(outgoing, "seq", split_axis=0, concat_axis=2, tiled=True)
+    arrived = _keep_up_series(outgoing, join_dim=0, dim_k=2)
     ordered = jnp.take(arrived[0], source, axis=1)
     return (ordered[0][None], ordered[1][None])
 

time: 190 us -> 203 us (1.068)
  waiting for transfers between devices: 95.5 us -> 55.6 us
  starting transfers between devices: 12.3 us -> 41.6 us
  local copies, waits for them, and re-layouts: 19.4 us -> 39.4 us
  other arithmetic: 14.5 us -> 16.9 us
    ppermute x3, waiting for transfers between devices: 95.5 us -> 7.86 us  [shifted(): return lax.ppermute(block, axis, route)]
    ppermute x0 -> x15, waiting for transfers between devices: none -> 47.8 us  [_keep_up_series(): block_out = lax.ppermute(block_out, bus_axis, items)]
    ppermute x0 -> x15, starting transfers between devices: none -> 34.1 us  [_keep_up_series(): block_out = lax.ppermute(block_out, bus_axis, items)]
    unnamed x18 -> x66, local copies, waits for them, and re-layouts: 6.28 us -> 21.7 us
    all_to_all x1 -> x0, starting transfers between devices: 6.57 us -> none  [hand_off(): lax.all_to_all(outgoing, 'seq', split_axis=0, concat_axis=2, tiled=True)]
    another operation x1 -> x3, local copies, waits for them, and re-layouts: 0.09 us -> 5.84 us
    dynamic_update_slice x0 -> x16, local copies, waits for them, and re-layouts: none -> 3.94 us  [_keep_up_series(): lax.dynamic_update_slice_in_dim(v1, block_out, (step_out ^ to_i) * main,...]
    all_to_all x1 -> x0, local copies, waits for them, and re-layouts: 3.23 us -> none  [hand_off(): lax.all_to_all(outgoing, 'seq', split_axis=0, concat_axis=2, tiled=True)]
  transfers between devices with their start and end apart: 4 -> 18, of which waited for: 3 -> 7; matrix products, arithmetic and copies ran while one was open for 9% -> 19% of each run, Pallas kernels for 0% -> 0%
where the time goes in v1:
time: 203 us; the launch traced here: 201 us
  waiting for transfers between devices  55.6 us (27%)
  matrix products  46.1 us (23%)
  starting transfers between devices  41.6 us (20%)
  local copies, waits for them, and re-layouts  39.4 us (19%)
  other arithmetic  16.9 us (8%)
    ppermute x15, waiting for transfers between devices, _keep_up_series(): block_out = lax.ppermute(block_out, bus_axis, items)  47.8 us
    ppermute x15, starting transfers between devices, _keep_up_series(): block_out = lax.ppermute(block_out, bus_axis, items)  34.1 us
    dot_general x16, matrix products, one_head(): jnp.einsum('qd,kd->qk', query_part, key_part, preferred_element_type=jnp....  24.7 us
    unnamed x66, local copies, waits for them, and re-layouts  21.7 us
    dot_general x16, matrix products, one_head(): jnp.dot(weights.astype(jnp.bfloat16), value_part, preferred_element_type=...  21.4 us
    ppermute x3, waiting for transfers between devices, shifted(): return lax.ppermute(block, axis, route)  7.86 us
    ppermute x3, starting transfers between devices, shifted(): return lax.ppermute(block, axis, route)  7.54 us
    another operation x2, local copies, waits for them, and re-layouts  5.59 us
  transfers between devices with their start and end apart: 18, of which 7 were waited for; matrix products, arithmetic and copies ran while one was open for 19% of the time, Pallas kernels for 0%

profile of v1, /device:TPU:20, one launch (start us, length us, event | category | flops | bytes accessed | tf_op | source)
XLA Modules:
  0.0 201.2 jit_solution(17770028794562548913)
XLA Ops:
  0.6 1.6 copy.35
  2.8 1.7 pad_maximum_fusion
  4.5 1.9 collective-permute-start
  8.3 5.5 %constant_dynamic-slice_fusion = (bf16[2,2,1,128,1,128]{5,4,3,1,2,0:T(2,128)(2,1)S(1)}, bf16[2,2,1,128,1,128]{5,4,3,1,2,0:T(2,128)(2,1)}, bf16[2,2,1,128,1,128]{...) fusion(bf16[2,2,1,128,16,128]{5,4,3,1,2,0:T(8,128)(2,1)S(1)} %c, ...), kind=kLoop, calls=%fused_computation.71 | loop fusion | bytes 4194368 | tf_op jit(solution)/shard_map/dynamic-slice.31
  14.5 1.6 collective-permute-start.3
  16.8 1.5 collective-permute-start.4
  19.0 1.4 collective-permute-start.6
  25.3 7.9 %collective-permute-done = bf16[2,256,2048]{1,2,0:T(8,128)(2,1)} collective-permute-done((bf16[2,256,2048]{1,2,0:T(8,128)(2,1)}, bf16[2,256,2048]{1,2,0:T(8,128)(2,1)}, u32[]{:S(2)}, u32[]{:S(2)}) %collective-permute-start) | collective-permute-done | bytes 2097184 | tf_op jit(solution)/shard_map/ppermute | solution.py:38
  33.2 2.8 %collective-permute-start.1 = (bf16[2,256,2048]{1,2,0:T(8,128)(2,1)}, bf16[2,256,2048]{1,2,0:T(8,128)(2,1)}, u32[]{:S(2)}, u32[]{:S(2)}) collective-permute-start(bf16[2,256,2048]{1,2,0:T(8,128)(2,1)} %collective-permute-done), channel_id=1, source_target_pairs={{0,1},{1,2},{2,3},{3,4},{4,5},{5,6},{6,7},{7,8},{8,9},{9,10},{10,1... | collective-permute-start | bytes 6291464 | tf_op jit(solution)/shard_map/ppermute | solution.py:38
  36.1 2.2 %copy.33 = bf16[256,2048]{0,1:T(8,128)(2,1)} copy(bf16[256,2048]{1,0:T(8,128)(2,1)} %param.9) | data formatting | bytes 2097152 | tf_op args[0]
  38.4 1.7 copy.91
  40.1 1.6 copy.90
  41.8 1.6 copy.89
  43.4 1.6 copy.88
  45.0 1.6 copy.87
  51.4 3.7 %collective-permute-start.7 = (bf16[1,2,2,128,128]{4,3,2,1,0:T(8,128)(2,1)}, bf16[1,2,2,128,128]{4,3,2,1,0:T(8,128)(2,1)S(1)}, u32[]{:S(2)}, u32[]{:S(2)}) collective-permute-start(bf16[1,2,2,128,128]{4,3,2,1,0:T(8,128)(2,1)} %bitcast.173), channel_id=1, source_target_pairs={{0,5},{1,4},{2,7},{3,6},{4,1},{5,0},{6,3},{7,2},{8,13},{9,12},{10,... | collective-permute-start | bytes 393224 | tf_op jit(solution)/shard_map/ppermute | solution.py:30
  60.4 3.9 %collective-permute-start.11 = (bf16[1,2,2,128,128]{4,3,2,1,0:T(8,128)(2,1)}, bf16[1,2,2,128,128]{4,3,2,1,0:T(8,128)(2,1)S(1)}, u32[]{:S(2)}, u32[]{:S(2)}) collective-permute-start(bf16[1,2,2,128,128]{4,3,2,1,0:T(8,128)(2,1)} %bitcast.169), channel_id=1, source_target_pairs={{0,9},{1,8},{2,11},{3,10},{4,13},{5,12},{6,15},{7,14},{8,1},{9,0},... | collective-permute-start | bytes 393224 | tf_op jit(solution)/shard_map/ppermute | solution.py:30
  65.1 8.2 %collective-permute-start.12 = (bf16[1,2,2,128,128]{4,3,2,1,0:T(8,128)(2,1)}, bf16[1,2,2,128,128]{4,3,2,1,0:T(8,128)(2,1)S(1)}, u32[]{:S(2)}, u32[]{:S(2)}) collective-permute-start(bf16[1,2,2,128,128]{4,3,2,1,0:T(8,128)(2,1)} %bitcast.168), channel_id=1, source_target_pairs={{0,10},{1,11},{2,8},{3,9},{4,14},{5,15},{6,12},{7,13},{8,2},{9,3},... | collective-permute-start | bytes 393224 | tf_op jit(solution)/shard_map/ppermute | solution.py:30
  73.5 1.5 collective-permute-start.14
  75.5 2.8 %collective-permute-start.2 = (bf16[2,256,2048]{1,2,0:T(8,128)(2,1)}, bf16[2,256,2048]{1,2,0:T(8,128)(2,1)}, u32[]{:S(2)}, u32[]{:S(2)}) collective-permute-start(bf16[2,256,2048]{1,2,0:T(8,128)(2,1)} %collective-permute-done.1), channel_id=1, source_target_pairs={{0,1},{1,2},{2,3},{3,4},{4,5},{5,6},{6,7},{7,8},{8,9},{9,10},{10,1... | collective-permute-start | bytes 6291464 | tf_op jit(solution)/shard_map/ppermute | solution.py:38
  78.3 7.6 %collective-permute-done.12 = bf16[1,2,2,128,128]{4,3,2,1,0:T(8,128)(2,1)S(1)} collective-permute-done((bf16[1,2,2,128,128]{4,3,2,1,0:T(8,128)(2,1)}, bf16[1,2,2,128,128]{4,3,2,1,0:T(8,128)(2,1)S(1)}, u32[]{:S(2)}, u32[]{:S(2)}) %collective-permute-start.12) | collective-permute-done | bytes 131104 | tf_op jit(solution)/shard_map/ppermute | solution.py:30
  86.0 4.1 %collective-permute-start.16 = (bf16[1,2,2,128,128]{4,3,2,1,0:T(8,128)(2,1)S(1)}, bf16[1,2,2,128,128]{4,3,2,1,0:T(8,128)(2,1)S(1)}, u32[]{:S(2)}, u32[]{:S(2)}) collective-permute-start(bf16[1,2,2,128,128]{4,3,2,1,0:T(8,128)(2,1)S(1)} %bitcast.164), channel_id=1, source_target_pairs={{0,14},{1,15},{2,12},{3,13},{4,10},{5,11},{6,8},{7,9},{8,6},{9,7},... | collective-permute-start | bytes 393224 | tf_op jit(solution)/shard_map/ppermute | solution.py:30
  90.2 6.0 %collective-permute-start.17 = (bf16[1,2,2,128,128]{4,3,2,1,0:T(8,128)(2,1)S(1)}, bf16[1,2,2,128,128]{4,3,2,1,0:T(8,128)(2,1)S(1)}, u32[]{:S(2)}, u32[]{:S(2)}) collective-permute-start(bf16[1,2,2,128,128]{4,3,2,1,0:T(8,128)(2,1)S(1)} %bitcast.163), channel_id=1, source_target_pairs={{0,15},{1,14},{2,13},{3,12},{4,11},{5,10},{6,9},{7,8},{8,7},{9,6},... | collective-permute-start | bytes 393224 | tf_op jit(solution)/shard_map/ppermute | solution.py:30
  96.2 6.7 %collective-permute-done.15 = bf16[1,2,2,128,128]{4,3,2,1,0:T(8,128)(2,1)S(1)} collective-permute-done((bf16[1,2,2,128,128]{4,3,2,1,0:T(8,128)(2,1)S(1)}, bf16[1,2,2,128,128]{4,3,2,1,0:T(8,128)(2,1)S(1)}, u32[]{:S(2)}, u32[]{:S(2)}) %collective-permute-start.15) | collective-permute-done | bytes 131104 | tf_op jit(solution)/shard_map/ppermute | solution.py:30
  103.0 3.8 %collective-permute-done.16 = bf16[1,2,2,128,128]{4,3,2,1,0:T(8,128)(2,1)S(1)} collective-permute-done((bf16[1,2,2,128,128]{4,3,2,1,0:T(8,128)(2,1)S(1)}, bf16[1,2,2,128,128]{4,3,2,1,0:T(8,128)(2,1)S(1)}, u32[]{:S(2)}, u32[]{:S(2)}) %collective-permute-start.16) | collective-permute-done | bytes 131104 | tf_op jit(solution)/shard_map/ppermute | solution.py:30
  106.8 28.7 %collective-permute-done.17 = bf16[1,2,2,128,128]{4,3,2,1,0:T(8,128)(2,1)S(1)} collective-permute-done((bf16[1,2,2,128,128]{4,3,2,1,0:T(8,128)(2,1)S(1)}, bf16[1,2,2,128,128]{4,3,2,1,0:T(8,128)(2,1)S(1)}, u32[]{:S(2)}, u32[]{:S(2)}) %collective-permute-start.17) | collective-permute-done | bytes 131104 | tf_op jit(solution)/shard_map/ppermute | solution.py:30
  135.5 2.2 %gather_fusion = bf16[32,2,128,128]{3,2,1,0:T(8,128)(2,1)} fusion(bf16[2,32,128,128]{3,2,1,0:T(8,128)(2,1)S(1)} %bitcast_dynamic-update-slice_fusion.1, s32[1024]{0:T(1024)S(1)} %pad_clamp_fusion), kind=kCustom, calls=%fused_computation | custom fusion | bytes 4194432 | tf_op jit(solution)/shard_map/jit(_take)/gather | solution.py:83
  137.6 1.8 select_bitcast_fusion
  139.5 1.5 slice_bitcast_fusion
  141.1 3.9 %maximum_maximum_fusion = bf16[2,1024,2048]{1,2,0:T(8,128)(2,1)S(1)} fusion(bf16[1,256,2048]{1,2,0:T(8,128)(2,1)S(1)} %bitcast.152, bf16[1,256,2048]{1,2,0:T(8,128)(2,1)S(1)} %bitcast.154, bf16[2,256,2048]{1,2,0:T(8,128)(2,1)} %collective-permute-done, bf16[2,256,2048]{1,2,0:T(8,128)(2,1)} %collective-permute-done.1, ...), kind=kLoop, calls=%fused_computation.22 | loop fusion | flops 41943040 | bytes 16777216 | tf_op jit(solution)/shard_map/concatenate | solution.py:96
  145.0 3.7 %fusion.26 = (bf16[1,1024,2048]{1,2,0:T(8,128)(2,1)}, bf16[1,1024,2048]{1,2,0:T(8,128)(2,1)}) fusion(bf16[2,1024,2048]{1,2,0:T(8,128)(2,1)S(1)} %maximum_maximum_fusion), kind=kLoop, calls=%fused_computation.117 | loop fusion | bytes 16777216 | tf_op jit(solution)/shard_map/slice | solution.py:121
  148.7 51.3 %while.11 = (s32[]{:T(128)}, bf16[16,256,128]{2,1,0:T(8,128)(2,1)S(1)}, bf16[16,256,128]{1,2,0:T(8,128)(2,1)}, bf16[16,1024,128]{1,2,0:T(8,128)(2,1)}, bf16[16,1...) while((s32[]{:T(128)}, ...), condition=%wide.region_9.10_spmd.clone, body=%wide.region_6.0_spmd.clone.sunk | while | flops 137133568 | bytes 3884141 | solution.py:138
  148.7 1.5 fusion.35
  151.9 1.5 fusion.35
  155.1 1.5 fusion.35
  158.3 1.5 fusion.35
  161.5 1.5 fusion.35
  164.7 1.5 fusion.35
  167.9 1.5 fusion.35
  171.1 1.5 fusion.35
  174.3 1.5 fusion.35
  177.5 1.5 fusion.35
  180.7 1.5 fusion.35
  183.9 1.5 fusion.35
  187.2 1.5 fusion.35
  190.4 1.5 fusion.35
  193.6 1.5 fusion.35
  196.8 1.5 fusion.35
  (154 shorter events, 48.5 us)
Async XLA Ops:
  0.6 1.6 copy-start.2
  2.8 1.7 copy-start
  4.5 28.7 %collective-permute-start = (bf16[2,256,2048]{1,2,0:T(8,128)(2,1)}, bf16[2,256,2048]{1,2,0:T(8,128)(2,1)}, u32[]{:S(2)}, u32[]{:S(2)}) collective-permute-start(bf16[2,256,2048]{1,2,0:T(8,128)(2,1)} %pad_maximum_fusion), channel_id=1, source_target_pairs={{0,1},{1,2},{2,3},{3,4},{4,5},{5,6},{6,7},{7,8},{8,9},{9,10},{10,1... | collective-permute-start | bytes 6291464 | tf_op jit(solution)/shard_map/ppermute | solution.py:38
  6.5 1.2 copy-start.3
  8.3 12.2 %copy-start.18 = (s32[8]{0:T(128)S(1)}, s32[8]{0:T(128)}, u32[]{:S(2)}) copy-start(s32[8]{0:T(128)} %param.12) | copy-start | bytes 100
  8.3 12.2 %copy-start.14 = (s32[16]{0:T(128)S(1)}, s32[16]{0:T(128)}, u32[]{:S(2)}) copy-start(s32[16]{0:T(128)} %param.14) | copy-start | bytes 196
  8.3 12.2 %copy-start.17 = (s32[16]{0:T(128)S(1)}, s32[16]{0:T(128)}, u32[]{:S(2)}) copy-start(s32[16]{0:T(128)} %param.13) | copy-start | bytes 196
  8.3 13.6 %copy-start.15 = (s32[8]{0:T(128)S(1)}, s32[8]{0:T(128)}, u32[]{:S(2)}) copy-start(s32[8]{0:T(128)} %param.15) | copy-start | bytes 100
  14.5 36.9 %collective-permute-start.3 = (bf16[1,2,2,128,128]{4,3,2,1,0:T(8,128)(2,1)}, bf16[1,2,2,128,128]{4,3,2,1,0:T(8,128)(2,1)}, u32[]{:S(2)}, u32[]{:S(2)}) collective-permute-start(bf16[1,2,2,128,128]{4,3,2,1,0:T(8,128)(2,1)} %bitcast.142), channel_id=1, source_target_pairs={{0,1},{1,0},{2,3},{3,2},{4,5},{5,4},{6,7},{7,6},{8,9},{9,8},{10,11... | collective-permute-start | bytes 393224 | tf_op jit(solution)/shard_map/ppermute | solution.py:30
  16.8 39.2 %collective-permute-start.4 = (bf16[1,2,2,128,128]{4,3,2,1,0:T(8,128)(2,1)}, bf16[1,2,2,128,128]{4,3,2,1,0:T(8,128)(2,1)}, u32[]{:S(2)}, u32[]{:S(2)}) collective-permute-start(bf16[1,2,2,128,128]{4,3,2,1,0:T(8,128)(2,1)} %bitcast.141), channel_id=1, source_target_pairs={{0,2},{1,3},{2,0},{3,1},{4,6},{5,7},{6,4},{7,5},{8,10},{9,11},{10,... | collective-permute-start | bytes 393224 | tf_op jit(solution)/shard_map/ppermute | solution.py:30
  19.0 38.9 %collective-permute-start.5 = (bf16[1,2,2,128,128]{4,3,2,1,0:T(8,128)(2,1)}, bf16[1,2,2,128,128]{4,3,2,1,0:T(8,128)(2,1)}, u32[]{:S(2)}, u32[]{:S(2)}) collective-permute-start(bf16[1,2,2,128,128]{4,3,2,1,0:T(8,128)(2,1)} %bitcast.140), channel_id=1, source_target_pairs={{0,3},{1,2},{2,1},{3,0},{4,7},{5,6},{6,5},{7,4},{8,11},{9,10},{10,... | collective-permute-start | bytes 393224 | tf_op jit(solution)/shard_map/ppermute | solution.py:30
  19.0 40.0 %collective-permute-start.6 = (bf16[1,2,2,128,128]{4,3,2,1,0:T(8,128)(2,1)S(1)}, bf16[1,2,2,128,128]{4,3,2,1,0:T(8,128)(2,1)}, u32[]{:S(2)}, u32[]{:S(2)}) collective-permute-start(bf16[1,2,2,128,128]{4,3,2,1,0:T(8,128)(2,1)S(1)} %bitcast.162), channel_id=1, source_target_pairs={{0,4},{1,5},{2,6},{3,7},{4,0},{5,1},{6,2},{7,3},{8,12},{9,13},{10,... | collective-permute-start | bytes 393224 | tf_op jit(solution)/shard_map/ppermute | solution.py:30
  21.8 3.5 %copy-start.10 = (bf16[2,2,1,128,1,128]{5,4,3,1,2,0:T(2,128)(2,1)S(1)}, bf16[2,2,1,128,1,128]{5,4,3,1,2,0:T(2,128)(2,1)}, u32[]{:S(2)}) copy-start(bf16[2,2,1,128,1,128]{5,4,3,1,2,0:T(2,128)(2,1)} %get-tuple-element.144) | copy-start | bytes 393220
  21.8 14.2 %copy-start.21 = (s32[2]{0:T(128)S(1)}, s32[2]{0:T(128)}, u32[]{:S(2)}) copy-start(s32[2]{0:T(128)} %dynamic_slice.69) | copy-start | bytes 28
  33.2 42.3 %collective-permute-start.1 = (bf16[2,256,2048]{1,2,0:T(8,128)(2,1)}, bf16[2,256,2048]{1,2,0:T(8,128)(2,1)}, u32[]{:S(2)}, u32[]{:S(2)}) collective-permute-start(bf16[2,256,2048]{1,2,0:T(8,128)(2,1)} %collective-permute-done), channel_id=1, source_target_pairs={{0,1},{1,2},{2,3},{3,4},{4,5},{5,6},{6,7},{7,8},{8,9},{9,10},{10,1... | collective-permute-start | bytes 6291464 | tf_op jit(solution)/shard_map/ppermute | solution.py:38
  38.4 8.3 %copy-start.9 = (bf16[2,2,1,128,1,128]{5,4,3,1,2,0:T(2,128)(2,1)S(1)}, bf16[2,2,1,128,1,128]{5,4,3,1,2,0:T(2,128)(2,1)}, u32[]{:S(2)}) copy-start(bf16[2,2,1,128,1,128]{5,4,3,1,2,0:T(2,128)(2,1)} %get-tuple-element.134) | copy-start | bytes 393220
  38.4 8.9 %copy-start.8 = (bf16[2,2,1,128,1,128]{5,4,3,1,2,0:T(2,128)(2,1)S(1)}, bf16[2,2,1,128,1,128]{5,4,3,1,2,0:T(2,128)(2,1)}, u32[]{:S(2)}) copy-start(bf16[2,2,1,128,1,128]{5,4,3,1,2,0:T(2,128)(2,1)} %get-tuple-element.133) | copy-start | bytes 393220
  38.4 9.6 %copy-start.7 = (bf16[2,2,1,128,1,128]{5,4,3,1,2,0:T(2,128)(2,1)S(1)}, bf16[2,2,1,128,1,128]{5,4,3,1,2,0:T(2,128)(2,1)}, u32[]{:S(2)}) copy-start(bf16[2,2,1,128,1,128]{5,4,3,1,2,0:T(2,128)(2,1)} %get-tuple-element.132) | copy-start | bytes 393220
  38.4 10.3 %copy-start.6 = (bf16[2,2,1,128,1,128]{5,4,3,1,2,0:T(2,128)(2,1)S(1)}, bf16[2,2,1,128,1,128]{5,4,3,1,2,0:T(2,128)(2,1)}, u32[]{:S(2)}) copy-start(bf16[2,2,1,128,1,128]{5,4,3,1,2,0:T(2,128)(2,1)} %get-tuple-element.131) | copy-start | bytes 393220
  38.4 10.9 %copy-start.5 = (bf16[2,2,1,128,1,128]{5,4,3,1,2,0:T(2,128)(2,1)S(1)}, bf16[2,2,1,128,1,128]{5,4,3,1,2,0:T(2,128)(2,1)}, u32[]{:S(2)}) copy-start(bf16[2,2,1,128,1,128]{5,4,3,1,2,0:T(2,128)(2,1)} %get-tuple-element.130) | copy-start | bytes 393220
  50.7 35.3 %copy-start.12 = (bf16[2,2,1,128,1,128]{5,3,4,1,2,0:T(8,128)(2,1)S(1)}, bf16[2,2,1,128,1,128]{5,3,4,1,2,0:T(8,128)(2,1)}, u32[]{:S(2)}) copy-start(bf16[2,2,1,128,1,128]{5,3,4,1,2,0:T(8,128)(2,1)} %copy.82) | copy-start | bytes 393220
  50.7 39.5 %copy-start.11 = (bf16[2,2,1,128,1,128]{5,3,4,1,2,0:T(8,128)(2,1)S(1)}, bf16[2,2,1,128,1,128]{5,3,4,1,2,0:T(8,128)(2,1)}, u32[]{:S(2)}) copy-start(bf16[2,2,1,128,1,128]{5,3,4,1,2,0:T(8,128)(2,1)} %copy.81) | copy-start | bytes 393220
  50.7 24.3 %copy-start.13 = (bf16[2,2,1,128,1,128]{5,3,4,1,2,0:T(8,128)(2,1)S(1)}, bf16[2,2,1,128,1,128]{5,3,4,1,2,0:T(8,128)(2,1)}, u32[]{:S(2)}) copy-start(bf16[2,2,1,128,1,128]{5,3,4,1,2,0:T(8,128)(2,1)} %copy.83) | copy-start | bytes 393220
  51.4 9.0 %collective-permute-start.7 = (bf16[1,2,2,128,128]{4,3,2,1,0:T(8,128)(2,1)}, bf16[1,2,2,128,128]{4,3,2,1,0:T(8,128)(2,1)S(1)}, u32[]{:S(2)}, u32[]{:S(2)}) collective-permute-start(bf16[1,2,2,128,128]{4,3,2,1,0:T(8,128)(2,1)} %bitcast.173), channel_id=1, source_target_pairs={{0,5},{1,4},{2,7},{3,6},{4,1},{5,0},{6,3},{7,2},{8,13},{9,12},{10,... | collective-permute-start | bytes 393224 | tf_op jit(solution)/shard_map/ppermute | solution.py:30
  56.0 9.2 %collective-permute-start.8 = (bf16[1,2,2,128,128]{4,3,2,1,0:T(8,128)(2,1)}, bf16[1,2,2,128,128]{4,3,2,1,0:T(8,128)(2,1)S(1)}, u32[]{:S(2)}, u32[]{:S(2)}) collective-permute-start(bf16[1,2,2,128,128]{4,3,2,1,0:T(8,128)(2,1)} %bitcast.172), channel_id=1, source_target_pairs={{0,6},{1,7},{2,4},{3,5},{4,2},{5,3},{6,0},{7,1},{8,14},{9,15},{10,... | collective-permute-start | bytes 393224 | tf_op jit(solution)/shard_map/ppermute | solution.py:30
  57.9 15.4 %collective-permute-start.9 = (bf16[1,2,2,128,128]{4,3,2,1,0:T(8,128)(2,1)}, bf16[1,2,2,128,128]{4,3,2,1,0:T(8,128)(2,1)S(1)}, u32[]{:S(2)}, u32[]{:S(2)}) collective-permute-start(bf16[1,2,2,128,128]{4,3,2,1,0:T(8,128)(2,1)} %bitcast.171), channel_id=1, source_target_pairs={{0,7},{1,6},{2,5},{3,4},{4,3},{5,2},{6,1},{7,0},{8,15},{9,14},{10,... | collective-permute-start | bytes 393224 | tf_op jit(solution)/shard_map/ppermute | solution.py:30
  59.0 14.4 %collective-permute-start.10 = (bf16[1,2,2,128,128]{4,3,2,1,0:T(8,128)(2,1)}, bf16[1,2,2,128,128]{4,3,2,1,0:T(8,128)(2,1)S(1)}, u32[]{:S(2)}, u32[]{:S(2)}) collective-permute-start(bf16[1,2,2,128,128]{4,3,2,1,0:T(8,128)(2,1)} %bitcast.170), channel_id=1, source_target_pairs={{0,8},{1,9},{2,10},{3,11},{4,12},{5,13},{6,14},{7,15},{8,0},{9,1},... | collective-permute-start | bytes 393224 | tf_op jit(solution)/shard_map/ppermute | solution.py:30
  60.4 14.6 %collective-permute-start.11 = (bf16[1,2,2,128,128]{4,3,2,1,0:T(8,128)(2,1)}, bf16[1,2,2,128,128]{4,3,2,1,0:T(8,128)(2,1)S(1)}, u32[]{:S(2)}, u32[]{:S(2)}) collective-permute-start(bf16[1,2,2,128,128]{4,3,2,1,0:T(8,128)(2,1)} %bitcast.169), channel_id=1, source_target_pairs={{0,9},{1,8},{2,11},{3,10},{4,13},{5,12},{6,15},{7,14},{8,1},{9,0},... | collective-permute-start | bytes 393224 | tf_op jit(solution)/shard_map/ppermute | solution.py:30
  65.1 20.8 %collective-permute-start.12 = (bf16[1,2,2,128,128]{4,3,2,1,0:T(8,128)(2,1)}, bf16[1,2,2,128,128]{4,3,2,1,0:T(8,128)(2,1)S(1)}, u32[]{:S(2)}, u32[]{:S(2)}) collective-permute-start(bf16[1,2,2,128,128]{4,3,2,1,0:T(8,128)(2,1)} %bitcast.168), channel_id=1, source_target_pairs={{0,10},{1,11},{2,8},{3,9},{4,14},{5,15},{6,12},{7,13},{8,2},{9,3},... | collective-permute-start | bytes 393224 | tf_op jit(solution)/shard_map/ppermute | solution.py:30
  73.4 16.8 %collective-permute-start.13 = (bf16[1,2,2,128,128]{4,3,2,1,0:T(8,128)(2,1)}, bf16[1,2,2,128,128]{4,3,2,1,0:T(8,128)(2,1)S(1)}, u32[]{:S(2)}, u32[]{:S(2)}) collective-permute-start(bf16[1,2,2,128,128]{4,3,2,1,0:T(8,128)(2,1)} %bitcast.167), channel_id=1, source_target_pairs={{0,11},{1,10},{2,9},{3,8},{4,15},{5,14},{6,13},{7,12},{8,3},{9,2},... | collective-permute-start | bytes 393224 | tf_op jit(solution)/shard_map/ppermute | solution.py:30
  73.5 22.7 %collective-permute-start.14 = (bf16[1,2,2,128,128]{4,3,2,1,0:T(8,128)(2,1)}, bf16[1,2,2,128,128]{4,3,2,1,0:T(8,128)(2,1)S(1)}, u32[]{:S(2)}, u32[]{:S(2)}) collective-permute-start(bf16[1,2,2,128,128]{4,3,2,1,0:T(8,128)(2,1)} %bitcast.166), channel_id=1, source_target_pairs={{0,12},{1,13},{2,14},{3,15},{4,8},{5,9},{6,10},{7,11},{8,4},{9,5},... | collective-permute-start | bytes 393224 | tf_op jit(solution)/shard_map/ppermute | solution.py:30
  75.0 27.9 %collective-permute-start.15 = (bf16[1,2,2,128,128]{4,3,2,1,0:T(8,128)(2,1)S(1)}, bf16[1,2,2,128,128]{4,3,2,1,0:T(8,128)(2,1)S(1)}, u32[]{:S(2)}, u32[]{:S(2)}) collective-permute-start(bf16[1,2,2,128,128]{4,3,2,1,0:T(8,128)(2,1)S(1)} %bitcast.165), channel_id=1, source_target_pairs={{0,13},{1,12},{2,15},{3,14},{4,9},{5,8},{6,11},{7,10},{8,5},{9,4},... | collective-permute-start | bytes 393224 | tf_op jit(solution)/shard_map/ppermute | solution.py:30
  75.5 65.4 %collective-permute-start.2 = (bf16[2,256,2048]{1,2,0:T(8,128)(2,1)}, bf16[2,256,2048]{1,2,0:T(8,128)(2,1)}, u32[]{:S(2)}, u32[]{:S(2)}) collective-permute-start(bf16[2,256,2048]{1,2,0:T(8,128)(2,1)} %collective-permute-done.1), channel_id=1, source_target_pairs={{0,1},{1,2},{2,3},{3,4},{4,5},{5,6},{6,7},{7,8},{8,9},{9,10},{10,1... | collective-permute-start | bytes 6291464 | tf_op jit(solution)/shard_map/ppermute | solution.py:38
  86.0 20.8 %collective-permute-start.16 = (bf16[1,2,2,128,128]{4,3,2,1,0:T(8,128)(2,1)S(1)}, bf16[1,2,2,128,128]{4,3,2,1,0:T(8,128)(2,1)S(1)}, u32[]{:S(2)}, u32[]{:S(2)}) collective-permute-start(bf16[1,2,2,128,128]{4,3,2,1,0:T(8,128)(2,1)S(1)} %bitcast.164), channel_id=1, source_target_pairs={{0,14},{1,15},{2,12},{3,13},{4,10},{5,11},{6,8},{7,9},{8,6},{9,7},... | collective-permute-start | bytes 393224 | tf_op jit(solution)/shard_map/ppermute | solution.py:30
  90.2 45.2 %collective-permute-start.17 = (bf16[1,2,2,128,128]{4,3,2,1,0:T(8,128)(2,1)S(1)}, bf16[1,2,2,128,128]{4,3,2,1,0:T(8,128)(2,1)S(1)}, u32[]{:S(2)}, u32[]{:S(2)}) collective-permute-start(bf16[1,2,2,128,128]{4,3,2,1,0:T(8,128)(2,1)S(1)} %bitcast.163), channel_id=1, source_target_pairs={{0,15},{1,14},{2,13},{3,12},{4,11},{5,10},{6,9},{7,8},{8,7},{9,6},... | collective-permute-start | bytes 393224 | tf_op jit(solution)/shard_map/ppermute | solution.py:30
  135.4 2.2 %copy-start.16 = (pred[32]{0:T(512)(128)(4,1)S(1)}, pred[32]{0:T(512)(128)(4,1)}, u32[]{:S(2)}) copy-start(pred[32]{0:T(512)(128)(4,1)} %compare_and_fusion) | copy-start | bytes 100
  139.5 1.6 copy-start.1
  145.0 3.7 %copy-start.4 = (bf16[16,256,128]{2,1,0:T(8,128)(2,1)S(1)}, bf16[16,256,128]{2,1,0:T(8,128)(2,1)}, u32[]{:S(2)}) copy-start(bf16[16,256,128]{2,1,0:T(8,128)(2,1)} %custom-call.3) | copy-start | bytes 3145732
  145.0 3.7 %copy-start.19 = (s32[256]{0:T(256)S(1)}, s32[256]{0:T(256)}, u32[]{:S(2)}) copy-start(s32[256]{0:T(256)} %broadcast_bitcast_fusion.1) | copy-start | bytes 3076
  145.0 3.7 %copy-start.20 = (pred[1024]{0:T(1024)(128)(4,1)S(1)}, pred[1024]{0:T(1024)(128)(4,1)}, u32[]{:S(2)}) copy-start(pred[1024]{0:T(1024)(128)(4,1)} %fusion.21) | copy-start | bytes 3076
